TPU v7x, 32 devices: a whole 2x2x4 slice. The times are simulated.
32 devices in a mesh: dp: 4 (over z), tensor: 8 (over y, x, core).
Axes of the slice: x: 2, y: 2, z: 4, core: 2. Of those that a mesh axis runs over, the one named last changes fastest.
Arguments:
- activations: bfloat16 [1024, 27648], P('dp', 'tensor'), may hold values from -6 to 6
- left_factor: float32 [216, 216], replicated, may hold values from -2 to 3, as said below
- right_factor: float32 [128, 128], replicated, may hold values from -2 to 3, as said below
- clip_scale: float32 [128, 216], replicated, may hold values from 0.5 to 3
- weight_rows: bfloat16 [27648, 5120], P('tensor'), may hold values from -0.0390625 to 0.0390625
- target: bfloat16 [1024, 5120], P('dp'), may hold values from -6 to 6
Outputs:
- grad_left: float32 [216, 216], replicated
- grad_right: float32 [128, 128], replicated
- grad_input: float32 [1024, 27648], P('dp', 'tensor')
Inputs may be any that keep to these rules, and one draw needn't show every extreme that they name: `left_factor`: the identity plus independent entries of order one over the square root of 216. `right_factor`: the identity plus independent entries of order one over the square root of 128.
All inputs are finite; a program needn't handle non-finite values.
Results may differ from a plain program's by a relative error of at most 0.007.
Values may be sent and summed in bfloat16 or wider, within the bound.
A program may use at most 128 MiB of HBM per device.

v0:
```python
import jax
import jax.numpy as jnp
from jax import lax
from jax.sharding import PartitionSpec as P


def local(activations, left_factor, right_factor, clip_scale, weight_rows, target):
    highest = lax.Precision.HIGHEST
    tok_rows = activations.shape[0]
    width_left = left_factor.shape[0]
    local_right = activations.shape[1] // width_left
    inputs = activations.reshape(tok_rows, local_right, width_left)
    moved = lax.all_to_all(inputs, "tensor", split_axis=0, concat_axis=1, tiled=True)
    mixed = jnp.einsum("tji,ik->tjk", moved.astype(jnp.float32), left_factor, precision=highest)
    rotated = jnp.einsum("jl,tjk->tlk", right_factor, mixed, precision=highest)
    bounded = jnp.tanh(rotated / clip_scale)
    clipped = (clip_scale * bounded).astype(jnp.bfloat16)
    clipped_back = lax.all_to_all(clipped, "tensor", split_axis=1, concat_axis=0, tiled=True)
    partial_out = jnp.dot(
        clipped_back.reshape(tok_rows, -1), weight_rows, preferred_element_type=jnp.float32
    )
    total = lax.psum(partial_out, "tensor")
    out_grad = (total - target.astype(jnp.float32)).astype(jnp.bfloat16)
    clipped_grad = lax.dot_general(
        out_grad, weight_rows, (((1,), (1,)), ((), ())), preferred_element_type=jnp.float32
    )
    clipped_grad = clipped_grad.reshape(tok_rows, local_right, width_left)
    grad_owned = lax.all_to_all(clipped_grad, "tensor", split_axis=0, concat_axis=1, tiled=True)
    rotated_grad = grad_owned * (1.0 - bounded * bounded)
    mixed_grad = jnp.einsum("jl,tlk->tjk", right_factor, rotated_grad, precision=highest)
    right_part = jnp.einsum("tjk,tlk->jl", mixed, rotated_grad, precision=highest)
    grad_back = lax.all_to_all(mixed_grad, "tensor", split_axis=1, concat_axis=0, tiled=True)
    input_grad = jnp.einsum("tjk,ik->tji", grad_back, left_factor, precision=highest).reshape(
        tok_rows, -1
    )
    left_part = jnp.einsum("tji,tjk->ik", inputs.astype(jnp.float32), grad_back, precision=highest)
    left_sum, right_sum = lax.psum((left_part, right_part), ("dp", "tensor"))
    return (left_sum, right_sum, input_grad)


def solution(mesh):
    placed = (P("dp", "tensor"), P(), P(), P(), P("tensor", None), P("dp", None))
    return jax.shard_map(
        local, mesh=mesh, in_specs=placed, out_specs=(P(), P(), P("dp", "tensor")), check_vma=False
    )
```

profile of v0, /device:TPU:8, one launch (start us, length us, event | category | flops | bytes accessed | tf_op | source)
XLA Modules:
  0.0 508.3 jit_solution(451690624203319944)
XLA Ops:
  7.2 0.0 copy-start
  7.2 0.0 all-reduce.4.cloned.1.call-start
  7.2 2.7 copy.31
  9.9 3.0 copy.32
  12.9 30.3 %all_to_all.69 = bf16[256,16,216]{2,1,0:T(8,128)(2,1)S(1)} all-to-all(bf16[256,16,216]{2,1,0:T(8,128)(2,1)} %copy.32), channel_id=1, replica_groups=mesh['dp'=4,'tensor'=8] {'tensor'}, dimensions={0} | all-to-all | bytes 3538944 | tf_op jit(solution)/shard_map/all_to_all | solution.py:13
  43.2 0.3 copy.33
  43.5 0.0 copy-start.2
  43.5 0.0 copy-start.3
  43.5 0.0 copy-done
  43.5 2.1 fusion.6
  45.7 0.0 copy-done.2
  45.7 0.0 copy-done.3
  45.7 0.0 copy-start.1
  45.7 4.7 multiply_convert_fusion
  50.4 0.0 copy-done.1
  50.4 4.5 copy.36
  54.9 30.1 %all_to_all.70 = bf16[32,128,216]{2,0,1:T(8,128)(2,1)S(1)} all-to-all(bf16[32,128,216]{2,0,1:T(8,128)(2,1)} %copy.36), channel_id=1, replica_groups=mesh['dp'=4,'tensor'=8] {'tensor'}, dimensions={1} | all-to-all | bytes 3538944 | tf_op jit(solution)/shard_map/all_to_all | solution.py:18
  85.0 2.6 copy.38
  87.6 5.2 %reshape.21 = bf16[256,3456]{1,0:T(8,128)(2,1)} reshape(bf16[8,32,16,216]{3,2,1,0:T(8,128)(2,1)} %copy.38) | data formatting | bytes 3538944 | tf_op jit(solution)/shard_map/reshape | solution.py:20
  92.8 18.0 %fusion.12 = f32[256,5120]{1,0:T(8,128)} fusion(bf16[256,3456]{1,0:T(8,128)(2,1)} %reshape.21, bf16[3456,5120]{1,0:T(8,128)(2,1)} %param.10), kind=kOutput, calls=%fused_computation.18 | convolution fusion | flops 9059696640 | bytes 42401792 | tf_op jit(solution)/shard_map/dot_general | solution.py:19
  110.8 0.0 all-reduce.4.cloned.1.call-update
  110.8 91.8 %all-reduce.4.cloned.1.call-done = f32[256,5120]{1,0:T(8,128)} async-done(((f32[256,5120]{1,0:T(8,128)}), f32[256,5120]{1,0:T(8,128)}) %all-reduce.4.cloned.1.call-update) | async-done | bytes 5242896 | tf_op jit(solution)/shard_map/psum | solution.py:22
  202.6 19.4 %fusion.1 = f32[256,3456]{0,1:T(8,128)} fusion(bf16[3456,5120]{1,0:T(8,128)(2,1)} %param.10, f32[256,5120]{1,0:T(8,128)} %all-reduce.4.cloned.1.call-done, bf16[256,5120]{1,0:T(8,128)(2,1)} %param.11), kind=kOutput, calls=%fused_computation.5 | convolution fusion | flops 9063628800 | bytes 46792704 | tf_op jit(solution)/shard_map/dot_general | solution.py:24
  222.0 5.3 %copy.40 = f32[256,16,216]{2,1,0:T(8,128)} copy(f32[256,16,216]{0,2,1:T(8,128)} %bitcast.63) | data formatting | bytes 7077888 | tf_op jit(solution)/shard_map/reshape | solution.py:27
  227.3 52.6 %all_to_all.71 = f32[256,16,216]{2,1,0:T(8,128)S(1)} all-to-all(f32[256,16,216]{2,1,0:T(8,128)} %copy.40), channel_id=1, replica_groups=mesh['dp'=4,'tensor'=8] {'tensor'}, dimensions={0} | all-to-all | bytes 7077888 | tf_op jit(solution)/shard_map/all_to_all | solution.py:28
  279.9 2.7 copy.41
  282.6 5.5 %copy.42 = f32[32,128,216]{1,2,0:T(8,128)} copy(f32[32,128,216]{2,1,0:T(8,128)} %bitcast.55) | data formatting | bytes 7077888 | tf_op jit(solution)/shard_map/all_to_all | solution.py:28
  288.1 6.4 %convolution_bitcast_fusion = f32[32,128,216]{1,2,0:T(8,128)} fusion(f32[32,128,216]{1,2,0:T(8,128)} %copy.42, f32[32,128,216]{1,2,0:T(8,128)} %get-tuple-element.15, f32[128,128]{1,0:T(8,128)S(1)} %copy-done.2), kind=kOutput, calls=%fused_computation.6 | convolution fusion | flops 1361608704 | bytes 10682368 | tf_op jit(solution)/shard_map/jl,tlk->tjk/dot_general | solution.py:30
  294.5 5.3 %copy.43 = f32[32,128,216]{2,0,1:T(8,128)} copy(f32[32,128,216]{1,2,0:T(8,128)} %convolution_bitcast_fusion) | data formatting | bytes 7077888 | tf_op jit(solution)/shard_map/jl,tlk->tjk/transpose | solution.py:30
  299.7 4.6 all-to-all-start.3
  304.3 0.3 all-reduce.6.cloned.1.call-start
  304.5 10.7 %fusion.3 = f32[128,128]{1,0:T(8,128)} fusion(f32[32,128,216]{1,2,0:T(8,128)} %copy-done.1, f32[32,128,216]{1,2,0:T(8,128)} %copy.42, f32[32,128,216]{1,2,0:T(8,128)} %get-tuple-element.15), kind=kOutput, calls=%fused_computation.9 | convolution fusion | flops 1361608704 | bytes 10682368 | tf_op jit(solution)/shard_map/tjk,tlk->jl/dot_general | solution.py:31
  315.3 38.1 %all-to-all-done.3 = f32[32,128,216]{2,0,1:T(8,128)} async-done(((f32[32,128,216]{2,0,1:T(8,128)}), f32[32,128,216]{2,0,1:T(8,128)}, u32[]{:S(2)}, u32[]{:S(2)}) %all-to-all-start.3) | async-done | bytes 3538976 | tf_op jit(solution)/shard_map/all_to_all | solution.py:32
  353.4 6.5 %copy.45 = f32[8,32,16,216]{3,2,1,0:T(8,128)} copy(f32[8,32,16,216]{3,1,2,0:T(8,128)} %bitcast.17) | data formatting | bytes 7077888 | tf_op jit(solution)/shard_map/all_to_all | solution.py:32
  359.9 5.1 %copy.46 = f32[256,16,216]{0,2,1:T(8,128)} copy(f32[256,16,216]{2,1,0:T(8,128)} %bitcast.56) | data formatting | bytes 7077888 | tf_op jit(solution)/shard_map/all_to_all | solution.py:32
  365.0 4.6 convolution_bitcast_fusion.1
  369.6 0.0 all-reduce.6.cloned.1.call-update
  369.6 7.1 %fusion.4 = f32[256,16,216]{0,2,1:T(8,128)} fusion(f32[256,16,216]{0,2,1:T(8,128)} %copy.46, f32[216,216]{1,0:T(8,128)S(1)} %copy-done), kind=kOutput, calls=%fused_computation.10 | convolution fusion | flops 2293235712 | bytes 7264512 | tf_op jit(solution)/shard_map/tjk,ik->tji/dot_general | solution.py:33
  376.7 5.2 %copy.49 = f32[256,3456]{1,0:T(8,128)} copy(f32[256,3456]{0,1:T(8,128)} %bitcast.59) | data formatting | bytes 7077888
  381.9 116.3 %all-reduce.6.cloned.1.call-done = (f32[216,216]{0,1:T(8,128)}, f32[128,128]{1,0:T(8,128)}) async-done(((f32[216,216]{0,1:T(8,128)}, f32[128,128]{1,0:T(8,128)}), (f32[216,216]{0,1:T(8,128)}, f32[128,128]{1,0:T(8,128)})) %all-reduce.6.cloned.1.call-update) | async-done | bytes 252176 | tf_op jit(solution)/shard_map/psum | solution.py:37
  498.2 1.7 copy.48
  499.9 1.5 copy.59
Async XLA Ops:
  7.2 36.4 %copy-start = (f32[216,216]{1,0:T(8,128)S(1)}, f32[216,216]{1,0:T(8,128)}, u32[]{:S(2)}) copy-start(f32[216,216]{1,0:T(8,128)} %param.7) | copy-start | bytes 559876
  7.2 195.4 %all-reduce.4.cloned.1.call-start = ((), (), s32[]{:S(2)}) async-start(), calls=%async_computation.4 | async-start | bytes 10485760 | tf_op jit(solution)/shard_map/psum | solution.py:22
  43.5 2.2 copy-start.2
  43.5 2.2 copy-start.3
  45.7 4.7 copy-start.1
  299.7 53.7 %all-to-all-start.3 = ((f32[32,128,216]{2,0,1:T(8,128)}), f32[32,128,216]{2,0,1:T(8,128)}, u32[]{:S(2)}, u32[]{:S(2)}) async-start(f32[32,128,216]{2,0,1:T(8,128)} %copy.43), calls=%async_computation.3 | async-start | bytes 8388608 | tf_op jit(solution)/shard_map/all_to_all | solution.py:32
  304.3 193.9 %all-reduce.6.cloned.1.call-start = ((), (), s32[]{:S(2)}) async-start(), calls=%async_computation.5 | async-start | bytes 573440 | tf_op jit(solution)/shard_map/psum | solution.py:37
Sparse Core Ops, SparseCore 0:
  110.9 91.6 all-reduce.3
  369.7 128.4 all-reduce.5
where the time goes:
time: 510 us; the launch traced here: 508 us
  waiting for transfers between devices  246 us (48%)
  blocking collectives  113 us (22%)
  matrix products  72.9 us (14%)
  local copies, waits for them, and re-layouts  57 us (11%)
  between operations  14.1 us (3%)
    psum x1, waiting for transfers between devices, local(): left_sum, right_sum = lax.psum((left_part, right_part), ('dp', 'tensor'))  116 us
    psum x1, waiting for transfers between devices, local(): total = lax.psum(partial_out, 'tensor')  91.8 us
    all_to_all x1, blocking collectives, local(): lax.all_to_all(clipped_grad, 'tensor', split_axis=0, concat_axis=1, tiled...  52.6 us
    all_to_all x1, waiting for transfers between devices, local(): lax.all_to_all(mixed_grad, 'tensor', split_axis=1, concat_axis=0, tiled=T...  38.1 us
    all_to_all x1, blocking collectives, local(): lax.all_to_all(inputs, 'tensor', split_axis=0, concat_axis=1, tiled=True)  30.3 us
    all_to_all x1, blocking collectives, local(): lax.all_to_all(clipped, 'tensor', split_axis=1, concat_axis=0, tiled=True)  30.1 us
    dot_general x1, matrix products, local(): lax.dot_general(out_grad, weight_rows, (((1,), (1,)), ((), ())), preferre...  19.4 us
    dot_general x1, matrix products, local(): jnp.dot(clipped_back.reshape(tok_rows, -1), weight_rows, preferred_elemen...  18 us
  transfers between devices with their start and end apart: 3, of which 3 were waited for; matrix products, arithmetic and copies ran while one was open for 5% of the time, Pallas kernels for 0%

commit v1 on v0

--- a/solution.py
+++ b/solution.py
@@ -2,6 +2,18 @@
 import jax.numpy as jnp
 from jax import lax
 from jax.sharding import PartitionSpec as P
+
+
+def views_enter(s0, dim_i, along_dim):
+    return jnp.concatenate(
+        jax.lax.all_to_all(
+            jnp.stack(jnp.split(s0, jax.lax.psum(1, axis_name="tensor"), axis=dim_i), axis=0),
+            axis_name="tensor",
+            split_axis=0,
+            concat_axis=0,
+        ),
+        axis=along_dim,
+    )
 
 
 def local(activations, left_factor, right_factor, clip_scale, weight_rows, target):
@@ -25,7 +37,7 @@
         out_grad, weight_rows, (((1,), (1,)), ((), ())), preferred_element_type=jnp.float32
     )
     clipped_grad = clipped_grad.reshape(tok_rows, local_right, width_left)
-    grad_owned = lax.all_to_all(clipped_grad, "tensor", split_axis=0, concat_axis=1, tiled=True)
+    grad_owned = views_enter(clipped_grad, 0, 1)
     rotated_grad = grad_owned * (1.0 - bounded * bounded)
     mixed_grad = jnp.einsum("jl,tlk->tjk", right_factor, rotated_grad, precision=highest)
     right_part = jnp.einsum("tjk,tlk->jl", mixed, rotated_grad, precision=highest)

time: 510 us -> 540 us (1.059)
  local copies, waits for them, and re-layouts: 57 us -> 81.5 us
    another operation x0 -> x9, local copies, waits for them, and re-layouts: none -> 16.1 us  [views_enter(): jnp.stack(jnp.split(s0, jax.lax.psum(1, axis_name='tensor'), axis=dim_i),...]
    unnamed x12 -> x23, local copies, waits for them, and re-layouts: 11.1 us -> 21.2 us
    all_to_all x2 -> x0, local copies, waits for them, and re-layouts: 8.18 us -> none  [local(): lax.all_to_all(clipped_grad, 'tensor', split_axis=0, concat_axis=1, tiled...]
  transfers between devices with their start and end apart: 3 -> 3, of which waited for: 3 -> 3; matrix products, arithmetic and copies ran while one was open for 5% -> 4% of each run, Pallas kernels for 0% -> 0%
where the time goes in v1:
time: 540 us; the launch traced here: 534 us
  waiting for transfers between devices  246 us (46%)
  blocking collectives  113 us (21%)
  local copies, waits for them, and re-layouts  81.5 us (15%)
  matrix products  74 us (14%)
  between operations  14.4 us (3%)
    psum x1, waiting for transfers between devices, local(): left_sum, right_sum = lax.psum((left_part, right_part), ('dp', 'tensor'))  116 us
    psum x1, waiting for transfers between devices, local(): total = lax.psum(partial_out, 'tensor')  91.8 us
    all_to_all x1, blocking collectives, views_enter(): jax.lax.all_to_all(jnp.stack(jnp.split(s0, jax.lax.psum(1, axis_name='ten...  52.6 us
    all_to_all x1, waiting for transfers between devices, local(): lax.all_to_all(mixed_grad, 'tensor', split_axis=1, concat_axis=0, tiled=T...  38.2 us
    all_to_all x1, blocking collectives, local(): lax.all_to_all(clipped, 'tensor', split_axis=1, concat_axis=0, tiled=True)  30.4 us
    all_to_all x1, blocking collectives, local(): lax.all_to_all(inputs, 'tensor', split_axis=0, concat_axis=1, tiled=True)  30.3 us
    unnamed x23, local copies, waits for them, and re-layouts  21.2 us
    dot_general x1, matrix products, local(): lax.dot_general(out_grad, weight_rows, (((1,), (1,)), ((), ())), preferre...  20.5 us
  transfers between devices with their start and end apart: 3, of which 3 were waited for; matrix products, arithmetic and copies ran while one was open for 4% of the time, Pallas kernels for 0%

profile of v1, /device:TPU:8, one launch (start us, length us, event | category | flops | bytes accessed | tf_op | source)
XLA Modules:
  0.0 534.4 jit_solution(17727284617664468298)
XLA Ops:
  7.2 0.0 all-reduce.4.cloned.1.call-start
  7.2 2.7 copy.44
  9.9 3.0 copy.45
  12.9 30.3 %all_to_all.56 = bf16[256,16,216]{2,1,0:T(8,128)(2,1)S(1)} all-to-all(bf16[256,16,216]{2,1,0:T(8,128)(2,1)} %copy.45), channel_id=1, replica_groups=mesh['dp'=4,'tensor'=8] {'tensor'}, dimensions={0} | all-to-all | bytes 3538944 | tf_op jit(solution)/shard_map/all_to_all | solution.py:25
  43.2 0.3 copy.46
  43.5 2.1 fusion.6
  45.7 4.7 multiply_convert_fusion
  50.4 4.5 copy.49
  54.9 30.4 %all_to_all.57 = bf16[32,128,216]{2,0,1:T(8,128)(2,1)S(1)} all-to-all(bf16[32,128,216]{2,0,1:T(8,128)(2,1)} %copy.49), channel_id=1, replica_groups=mesh['dp'=4,'tensor'=8] {'tensor'}, dimensions={1} | all-to-all | bytes 3538944 | tf_op jit(solution)/shard_map/all_to_all | solution.py:30
  85.3 2.6 copy.51
  87.9 5.1 reshape.41
  93.0 17.9 %fusion.13 = f32[256,5120]{1,0:T(8,128)} fusion(bf16[256,3456]{1,0:T(8,128)(2,1)} %reshape.41, bf16[3456,5120]{1,0:T(8,128)(2,1)} %param.10), kind=kOutput, calls=%fused_computation.27 | convolution fusion | flops 9059696640 | bytes 42401792 | tf_op jit(solution)/shard_map/dot_general | solution.py:31
  111.0 91.8 %all-reduce.4.cloned.1.call-done = f32[256,5120]{1,0:T(8,128)} async-done(((f32[256,5120]{1,0:T(8,128)}), f32[256,5120]{1,0:T(8,128)}) %all-reduce.4.cloned.1.call-update) | async-done | bytes 5242896 | tf_op jit(solution)/shard_map/psum | solution.py:34
  202.8 20.5 %fusion.1 = f32[256,3456]{1,0:T(8,128)} fusion(bf16[3456,5120]{1,0:T(8,128)(2,1)} %param.10, f32[256,5120]{1,0:T(8,128)} %all-reduce.4.cloned.1.call-done, bf16[256,5120]{1,0:T(8,128)(2,1)} %param.11), kind=kOutput, calls=%fused_computation.5 | convolution fusion | flops 9063628800 | bytes 46792704 | tf_op jit(solution)/shard_map/dot_general | solution.py:36
  223.3 3.5 fusion.12
  226.9 1.8 stack.27
  228.7 0.8 constant_dynamic-update-slice_fusion.7
  229.5 2.6 stack.28
  232.1 2.6 stack.29
  234.7 2.6 stack.30
  237.3 2.6 stack.31
  239.9 1.6 stack.32
  241.5 0.8 stack.33
  242.3 0.8 stack.34
  243.0 1.9 constant_dynamic-update-slice_fusion.6
  245.0 1.9 constant_dynamic-update-slice_fusion.5
  246.9 1.9 constant_dynamic-update-slice_fusion.4
  248.7 1.9 constant_dynamic-update-slice_fusion.3
  250.6 0.8 constant_dynamic-update-slice_fusion.2
  251.5 0.9 constant_dynamic-update-slice_fusion.1
  252.3 0.8 constant_dynamic-update-slice_fusion
  253.2 52.6 %all_to_all.58 = f32[8,32,16,216]{3,2,1,0:T(8,128)S(1)} all-to-all(f32[8,32,16,216]{3,2,1,0:T(8,128)} %constant_dynamic-update-slice_fusion), channel_id=1, replica_groups=mesh['dp'=4,'tensor'=8] {'tensor'}, dimensions={0} | all-to-all | bytes 7077888 | tf_op jit(solution)/shard_map/all_to_all | solution.py:9
  305.8 2.6 copy.52
  308.4 5.4 %copy.53 = f32[32,128,216]{1,2,0:T(8,128)} copy(f32[32,128,216]{2,1,0:T(8,128)} %bitcast.52) | data formatting | bytes 7077888 | tf_op jit(solution)/shard_map/reshape | solution.py:8
  313.8 6.3 %convolution_bitcast_fusion = f32[32,128,216]{1,2,0:T(8,128)} fusion(f32[32,128,216]{1,2,0:T(8,128)} %copy.53, f32[32,128,216]{1,2,0:T(8,128)} %get-tuple-element.23, f32[128,128]{1,0:T(8,128)S(1)} %copy-done.4), kind=kOutput, calls=%fused_computation.6 | convolution fusion | flops 1361608704 | bytes 10682368 | tf_op jit(solution)/shard_map/jl,tlk->tjk/dot_general | solution.py:42
  320.2 5.2 copy.54
  325.4 4.6 all-to-all-start.3
  330.0 0.2 all-reduce.6.cloned.1.call-start
  330.2 10.7 %fusion.3 = f32[128,128]{1,0:T(8,128)} fusion(f32[32,128,216]{1,2,0:T(8,128)} %copy-done.1, f32[32,128,216]{1,2,0:T(8,128)} %copy.53, f32[32,128,216]{1,2,0:T(8,128)} %get-tuple-element.23), kind=kOutput, calls=%fused_computation.9 | convolution fusion | flops 1361608704 | bytes 10682368 | tf_op jit(solution)/shard_map/tjk,tlk->jl/dot_general | solution.py:43
  340.9 38.2 %all-to-all-done.3 = f32[32,128,216]{2,0,1:T(8,128)} async-done(((f32[32,128,216]{2,0,1:T(8,128)}), f32[32,128,216]{2,0,1:T(8,128)}, u32[]{:S(2)}, u32[]{:S(2)}) %all-to-all-start.3) | async-done | bytes 3538976 | tf_op jit(solution)/shard_map/all_to_all | solution.py:44
  379.1 6.6 %copy.56 = f32[8,32,16,216]{3,2,1,0:T(8,128)} copy(f32[8,32,16,216]{3,1,2,0:T(8,128)} %bitcast.15) | data formatting | bytes 7077888 | tf_op jit(solution)/shard_map/all_to_all | solution.py:44
  385.6 5.3 copy.57
  390.9 4.6 convolution_bitcast_fusion.1
  395.5 7.1 %fusion.4 = f32[256,16,216]{0,2,1:T(8,128)} fusion(f32[256,16,216]{0,2,1:T(8,128)} %copy.57, f32[216,216]{1,0:T(8,128)S(1)} %copy-done), kind=kOutput, calls=%fused_computation.10 | convolution fusion | flops 2293235712 | bytes 7264512 | tf_op jit(solution)/shard_map/tjk,ik->tji/dot_general | solution.py:45
  402.6 5.2 copy.60
  407.8 116.3 %all-reduce.6.cloned.1.call-done = (f32[216,216]{0,1:T(8,128)}, f32[128,128]{1,0:T(8,128)}) async-done(((f32[216,216]{0,1:T(8,128)}, f32[128,128]{1,0:T(8,128)}), (f32[216,216]{0,1:T(8,128)}, f32[128,128]{1,0:T(8,128)})) %all-reduce.6.cloned.1.call-update) | async-done | bytes 252176 | tf_op jit(solution)/shard_map/psum | solution.py:49
  524.1 1.7 copy.59
  525.9 1.5 copy.76
  (14 shorter events, 0.1 us)
Async XLA Ops:
  7.2 36.4 %copy-start = (f32[216,216]{1,0:T(8,128)S(1)}, f32[216,216]{1,0:T(8,128)}, u32[]{:S(2)}) copy-start(f32[216,216]{1,0:T(8,128)} %param.7) | copy-start | bytes 559876
  7.2 195.6 %all-reduce.4.cloned.1.call-start = ((), (), s32[]{:S(2)}) async-start(), calls=%async_computation.4 | async-start | bytes 10485760 | tf_op jit(solution)/shard_map/psum | solution.py:34
  43.5 2.2 copy-start.4
  43.5 2.2 copy-start.5
  45.7 4.7 copy-start.1
  229.5 10.4 %copy-start.3 = (f32[32,3456]{1,0:T(8,128)S(1)}, f32[32,3456]{1,0:T(8,128)}, u32[]{:S(2)}) copy-start(f32[32,3456]{1,0:T(8,128)} %get-tuple-element.16) | copy-start | bytes 1327108
  243.0 7.6 %copy-start.2 = (f32[1,32,16,216]{3,2,1,0:T(8,128)S(1)}, f32[1,32,16,216]{3,2,1,0:T(8,128)}, u32[]{:S(2)}) copy-start(f32[1,32,16,216]{3,2,1,0:T(8,128)} %stack.32) | copy-start | bytes 1327108
  325.4 53.7 %all-to-all-start.3 = ((f32[32,128,216]{2,0,1:T(8,128)}), f32[32,128,216]{2,0,1:T(8,128)}, u32[]{:S(2)}, u32[]{:S(2)}) async-start(f32[32,128,216]{2,0,1:T(8,128)} %copy.54), calls=%async_computation.3 | async-start | bytes 8388608 | tf_op jit(solution)/shard_map/all_to_all | solution.py:44
  330.0 194.2 %all-reduce.6.cloned.1.call-start = ((), (), s32[]{:S(2)}) async-start(), calls=%async_computation.5 | async-start | bytes 573440 | tf_op jit(solution)/shard_map/psum | solution.py:49
Sparse Core Ops, SparseCore 0:
  111.1 91.6 all-reduce.3
  395.6 128.4 all-reduce.5
